TPU v7x, 32 devices: a whole 2x2x4 slice. The times are simulated.
32 devices in a mesh: row: 16 (over z, x, core), col: 2 (over y).
Axes of the slice: x: 2, y: 2, z: 4, core: 2. Of those that a mesh axis runs over, the one named last changes fastest.
Arguments:
- species: float32 [2, 128, 128, 64], P(None, None, 'row', 'col'), may hold values from -6 to 6
- symbol_x: float32 [128], replicated, may hold values from 0.3 to 3
- symbol_y: float32 [128], replicated, may hold values from 0.3 to 3
- symbol_z: float32 [64], replicated, may hold values from 0.3 to 3
Outputs:
- spectrum: float32 [2, 128, 128, 64], P(None, 'row', 'col')
All inputs are finite; a program needn't handle non-finite values.
Results may differ from a plain program's by a relative error of at most 0.00007.
Values sent between devices are 32-bit elements; how exact they have to be, the bound alone decides.
No kernel may reach another device: no remote copies, remote signals or barrier semaphores. Data moves between devices by JAX's collectives and lax.ppermute only.
A program may use at most 64 MiB of HBM per device.

v0:
```python
import jax
import jax.numpy as jnp
from jax import lax
from jax.sharding import PartitionSpec as P


def basis_table(count):
    rank = jnp.arange(count)
    angle = (
        jnp.pi
        / (4 * count)
        * ((2 * rank[:, None] + 1) * (2 * rank[None, :] + 1) % (8 * count)).astype(jnp.float32)
    )
    return jnp.cos(angle) * (2.0 / count) ** 0.5


def to_modes(values, dim):
    moved = jnp.tensordot(
        values, basis_table(values.shape[dim]), axes=([dim], [0]), precision=lax.Precision.HIGHEST
    )
    return jnp.moveaxis(moved, -1, dim)


def on_device(species, symbol_x, symbol_y, symbol_z):
    part_values = species
    part_values = to_modes(part_values, 1)
    part_values = lax.all_to_all(part_values, "row", split_axis=1, concat_axis=2, tiled=True)
    part_values = to_modes(part_values, 2)
    local_values = part_values
    local_values = lax.all_to_all(local_values, "col", split_axis=2, concat_axis=3, tiled=True)
    local_values = to_modes(local_values, 3)
    share_x = local_values.shape[1]
    part_x = lax.dynamic_slice_in_dim(symbol_x, lax.axis_index("row") * share_x, share_x)
    share_y = local_values.shape[2]
    part_y = lax.dynamic_slice_in_dim(symbol_y, lax.axis_index("col") * share_y, share_y)
    symbol = part_x[:, None, None] + part_y[None, :, None] + symbol_z[None, None, :]
    local_values = local_values / symbol
    return local_values


def solution(mesh):
    in_specs = (P(None, None, "row", "col"), P(), P(), P())
    out_specs = P(None, "row", "col", None)
    return jax.shard_map(
        on_device, mesh=mesh, in_specs=in_specs, out_specs=out_specs, check_vma=False
    )
```

profile of v0, /device:TPU:0, one launch (start us, length us, event | category | flops | bytes accessed | tf_op | source)
XLA Modules:
  0.0 39.9 jit_solution(311103156641426891)
XLA Ops:
  0.0 0.9 %copy-done = f32[2,128,8,32]{1,3,2,0:T(8,128)S(1)} copy-done((f32[2,128,8,32]{1,3,2,0:T(8,128)S(1)}, f32[2,128,8,32]{1,3,2,0:T(8,128)}, u32[]{:S(2)}) %copy-start) | copy-done | bytes 262168
  1.0 0.7 %fusion.16 = f32[128,512]{0,1:S(1)} fusion(f32[128,512]{0,1:T(8,128)S(1)} %bitcast.33, s32[128]{0:T(128)S(1)} %multiply_add_fusion.1), kind=kOutput, calls=%fused_computation.27 | convolution fusion | flops 100909056 | bytes 524800
  1.6 0.5 %copy.18 = f32[2,128,8,32]{3,2,0,1:T(8,128)S(1)} copy(f32[2,128,8,32]{1,3,2,0:T(8,128)S(1)} %bitcast.39) | data formatting | bytes 524288 | tf_op jit(solution)/shard_map/transpose | solution.py:21
  2.1 1.2 %reshape.66 = f32[16,1,4096]{2,1,0:T(1,128)} reshape(f32[128,2,8,32]{3,2,1,0:T(8,128)S(1)} %bitcast.34) | data formatting | bytes 524288
  3.3 7.4 %all-to-all-start = ((f32[16,1,4096]{2,1,0:T(1,128)}), f32[16,1,4096]{2,1,0:T(1,128)S(1)}, u32[]{:S(2)}, u32[]{:S(2)}) async-start(f32[16,1,4096]{2,1,0:T(1,128)} %reshape.66), calls=%async_computation | async-start | bytes 524288 | tf_op jit(solution)/shard_map/all_to_all | solution.py:27
  10.7 0.6 %copy-done.2 = f32[128]{0:T(128)S(1)} copy-done((f32[128]{0:T(128)S(1)}, f32[128]{0:T(128)}, u32[]{:S(2)}) %copy-start.2) | copy-done | bytes 536
  11.4 0.1 dynamic_slice.7
  11.4 0.7 %copy-done.3 = f32[128]{0:T(128)S(1)} copy-done((f32[128]{0:T(128)S(1)}, f32[128]{0:T(128)}, u32[]{:S(2)}) %copy-start.3) | copy-done | bytes 536
  12.1 0.1 dynamic_slice.6
  12.2 0.1 broadcast_add_fusion.1
  12.2 8.5 %all-to-all-done = f32[16,1,4096]{2,1,0:T(1,128)S(1)} async-done(((f32[16,1,4096]{2,1,0:T(1,128)}), f32[16,1,4096]{2,1,0:T(1,128)S(1)}, u32[]{:S(2)}, u32[]{:S(2)}) %all-to-all-start) | async-done | bytes 262176 | tf_op jit(solution)/shard_map/all_to_all | solution.py:27
  20.7 0.6 %broadcast.126 = f32[]{:T(128)} broadcast(f32[]{:T(128)} %constant.114), dimensions={} | broadcast | bytes 8 | tf_op jit(solution)/shard_map/all_to_all | solution.py:27
  21.3 1.2 %reduce = f32[16,4096]{1,0:T(8,128)S(1)} reduce(f32[16,1,4096]{2,1,0:T(1,128)S(1)} %all-to-all-done, f32[]{:T(128)} %broadcast.126), dimensions={1}, to_apply=%all_to_all.26.reduce_sub_computation | reduce | bytes 524292 | tf_op jit(solution)/shard_map/all_to_all | solution.py:27
  22.5 0.3 reshape.67
  22.9 1.9 %convolution_bitcast_fusion = f32[2,8,128,32]{2,3,1,0:T(8,128)S(1)} fusion(f32[2,8,16,8,32]{4,3,0,1,2:T(8,128)S(1)} %bitcast.37, s32[128]{0:T(128)S(1)} %multiply_add_fusion.1), kind=kOutput, calls=%fused_computation.1 | convolution fusion | flops 100909056 | bytes 524800 | tf_op jit(solution)/shard_map/dot_general | solution.py:18
  24.8 0.5 %copy.22 = f32[2,8,128,32]{3,1,0,2:T(8,128)S(1)} copy(f32[2,8,128,32]{2,3,1,0:T(8,128)S(1)} %convolution_bitcast_fusion) | data formatting | bytes 524288 | tf_op jit(solution)/shard_map/transpose | solution.py:21
  25.3 1.2 %reshape.68 = f32[2,1,32768]{2,1,0:T(1,128)} reshape(f32[128,2,8,32]{3,2,1,0:T(8,128)S(1)} %bitcast.35) | data formatting | bytes 524288
  26.5 3.6 %all-to-all-start.1 = ((f32[2,1,32768]{2,1,0:T(1,128)}), f32[2,1,32768]{2,1,0:T(1,128)S(1)}, u32[]{:S(2)}, u32[]{:S(2)}) async-start(f32[2,1,32768]{2,1,0:T(1,128)} %reshape.68), calls=%async_computation.1 | async-start | bytes 524288 | tf_op jit(solution)/shard_map/all_to_all | solution.py:30
  30.1 0.1 broadcast_add_fusion
  30.2 5.3 %all-to-all-done.1 = f32[2,1,32768]{2,1,0:T(1,128)S(1)} async-done(((f32[2,1,32768]{2,1,0:T(1,128)}), f32[2,1,32768]{2,1,0:T(1,128)S(1)}, u32[]{:S(2)}, u32[]{:S(2)}) %all-to-all-start.1) | async-done | bytes 262176 | tf_op jit(solution)/shard_map/all_to_all | solution.py:30
  35.6 1.4 %reduce.1 = f32[2,32768]{1,0:T(2,128)S(1)} reduce(f32[2,1,32768]{2,1,0:T(1,128)S(1)} %all-to-all-done.1, f32[]{:T(128)} %broadcast.126), dimensions={1}, to_apply=%all_to_all.30.reduce_sub_computation | reduce | bytes 524292 | tf_op jit(solution)/shard_map/all_to_all | solution.py:30
  37.0 0.5 %reshape.69 = f32[128,2,8,32]{3,2,1,0:T(8,128)S(1)} reshape(f32[2,32768]{1,0:T(2,128)S(1)} %reduce.1) | data formatting | bytes 524288
  37.5 0.5 %copy.31 = f32[2,8,2,64,32]{3,2,4,1,0:T(2,128)S(1)} copy(f32[2,8,2,64,32]{4,1,0,3,2:T(8,128)S(1)} %bitcast.36) | data formatting | bytes 524288 | tf_op jit(solution)/shard_map/all_to_all | solution.py:30
  38.0 1.8 %convolution_divide_fusion = f32[2,8,64,64]{3,2,1,0:T(8,128)} fusion(f32[2,8,64,64]{2,3,1,0:T(8,128)S(1)} %bitcast.40, f32[8,64,64]{2,1,0:T(8,128)S(1)} %broadcast_add_fusion, s32[64]{0:T(128)S(1)} %multiply_add_fusion), kind=kOutput, calls=%fused_computation | convolution fusion | flops 50458624 | bytes 655616 | tf_op jit(solution)/shard_map/dot_general | solution.py:18
  (8 shorter events, 0.1 us)
Async XLA Ops:
  0.0 1.0 %copy-start = (f32[2,128,8,32]{1,3,2,0:T(8,128)S(1)}, f32[2,128,8,32]{1,3,2,0:T(8,128)}, u32[]{:S(2)}) copy-start(f32[2,128,8,32]{1,3,2,0:T(8,128)} %param.4) | copy-start | bytes 786436
  3.3 17.4 %all-to-all-start = ((f32[16,1,4096]{2,1,0:T(1,128)}), f32[16,1,4096]{2,1,0:T(1,128)S(1)}, u32[]{:S(2)}, u32[]{:S(2)}) async-start(f32[16,1,4096]{2,1,0:T(1,128)} %reshape.66), calls=%async_computation | async-start | bytes 524288 | tf_op jit(solution)/shard_map/all_to_all | solution.py:27
  10.7 0.7 %copy-start.2 = (f32[128]{0:T(128)S(1)}, f32[128]{0:T(128)}, u32[]{:S(2)}) copy-start(f32[128]{0:T(128)} %param.6) | copy-start | bytes 1540
  11.4 0.7 %copy-start.3 = (f32[128]{0:T(128)S(1)}, f32[128]{0:T(128)}, u32[]{:S(2)}) copy-start(f32[128]{0:T(128)} %param.5) | copy-start | bytes 1540
  26.5 3.6 %copy-start.1 = (f32[64]{0:T(128)S(1)}, f32[64]{0:T(128)}, u32[]{:S(2)}) copy-start(f32[64]{0:T(128)} %param.7) | copy-start | bytes 772
  26.5 9.1 %all-to-all-start.1 = ((f32[2,1,32768]{2,1,0:T(1,128)}), f32[2,1,32768]{2,1,0:T(1,128)S(1)}, u32[]{:S(2)}, u32[]{:S(2)}) async-start(f32[2,1,32768]{2,1,0:T(1,128)} %reshape.68), calls=%async_computation.1 | async-start | bytes 524288 | tf_op jit(solution)/shard_map/all_to_all | solution.py:30
where the time goes:
time: 40.2 us; the launch traced here: 39.9 us
  waiting for transfers between devices  13.8 us (34%)
  starting transfers between devices  11 us (27%)
  local copies, waits for them, and re-layouts  7.65 us (19%)
  matrix products  4.44 us (11%)
  other arithmetic  2.88 us (7%)
    all_to_all x1, waiting for transfers between devices, on_device(): lax.all_to_all(part_values, 'row', split_axis=1, concat_axis=2, tiled=True)  8.47 us
    all_to_all x1, starting transfers between devices, on_device(): lax.all_to_all(part_values, 'row', split_axis=1, concat_axis=2, tiled=True)  7.39 us
    unnamed x12, local copies, waits for them, and re-layouts  5.37 us
    all_to_all x1, waiting for transfers between devices, on_device(): lax.all_to_all(local_values, 'col', split_axis=2, concat_axis=3, tiled=True)  5.35 us
    dot_general x2, matrix products, to_modes(): jnp.tensordot(values, basis_table(values.shape[dim]), axes=([dim], [0]),...  3.76 us
    all_to_all x1, starting transfers between devices, on_device(): lax.all_to_all(local_values, 'col', split_axis=2, concat_axis=3, tiled=True)  3.58 us
    all_to_all x1, other arithmetic, on_device(): lax.all_to_all(local_values, 'col', split_axis=2, concat_axis=3, tiled=True)  1.43 us
    all_to_all x1, other arithmetic, on_device(): lax.all_to_all(part_values, 'row', split_axis=1, concat_axis=2, tiled=True)  1.25 us
  transfers between devices with their start and end apart: 2, of which 2 were waited for; matrix products, arithmetic and copies ran while one was open for 1% of the time, Pallas kernels for 0%

commit v1 on v0

v1 whole, which is shorter than its diff:
```python
import functools

import jax
import jax.numpy as jnp
import numpy as np
from jax import lax
from jax.experimental import pallas as pl
from jax.experimental.pallas import tpu as pltpu
from jax.sharding import PartitionSpec as P

LANES = 128
SUBLANES = 8
VMEM_GRANT = 12 * 2**20
VMEM = pl.BlockSpec(memory_space=pltpu.VMEM)
SMEM = pl.BlockSpec(memory_space=pltpu.SMEM)


def basis_table(count):
    rank = np.arange(count)
    odd = 2 * rank + 1
    angle = np.pi / (4 * count) * (odd[:, None] * odd[None, :] % (8 * count))
    return (np.cos(angle) * (2.0 / count) ** 0.5).astype(np.float32)


def split_table(table):
    high = table.astype(jnp.bfloat16)
    low = (table - high.astype(np.float32)).astype(jnp.bfloat16)
    return high, low


def split(values):
    high = values.astype(jnp.bfloat16)
    low = (values - high.astype(jnp.float32)).astype(jnp.bfloat16)
    return high, low


def dot(left, right):
    return jnp.dot(left, right, preferred_element_type=jnp.float32)


def dot_nt(left, right):
    return lax.dot_general(
        left, right, (((1,), (1,)), ((), ())), preferred_element_type=jnp.float32
    )


def x_kernel(a_ref, h_ref, o_ref):
    fields, ys, zs, _ = a_ref.shape
    half = fields * zs
    parts = LANES // half
    rows = h_ref.shape[0] // parts
    table = h_ref[...]
    lane = lax.broadcasted_iota(jnp.int32, (rows, LANES), 1)
    for y in range(ys):
        a = jnp.concatenate([a_ref[f, y] for f in range(fields)] * parts, axis=0)
        high, low = split(a)
        c = dot_nt(table, jnp.concatenate([high, high, low], axis=1))
        out = c[:rows]
        for part in range(1, parts):
            out = jnp.where(lane < part * half, out, c[part * rows : (part + 1) * rows])
        o_ref[pl.ds(y, rows, stride=ys), :] = out


def y_products(r_ref, table):
    count, k_lo, ys, lanes = r_ref.shape
    outs = []
    for k in range(k_lo):
        r = r_ref[:, k].reshape(count * ys, lanes)
        high, low = split(r)
        outs.append(dot(table, jnp.concatenate([high, high, low], axis=0)))
    return outs


def y_send_kernel(cols, r_ref, h_ref, *o_refs):
    me = lax.axis_index("col")
    for step, o_ref in enumerate(o_refs, 1):
        target = lax.rem(me + step, cols)
        for k, out in enumerate(y_products(r_ref, h_ref[target])):
            o_ref[k] = out


def y_keep_kernel(cols, r_ref, h_ref, w_ref, sx_ref, sy_ref, sz_ref, o_ref, inv_ref, sy_scr):
    me = lax.axis_index("col")
    row = lax.axis_index("row")
    fields, share_x, share_y, nz = o_ref.shape
    k_lo = r_ref.shape[1]
    parts = share_x // k_lo
    ny = sy_ref.shape[1]
    for i in range(ny // LANES):
        sy_scr[i * LANES : (i + 1) * LANES, :] = jnp.broadcast_to(
            sy_ref[:, i * LANES : (i + 1) * LANES], (LANES, LANES)
        ).T
    sy = sy_scr[pl.ds(me * share_y, share_y), :][:, :1]
    sz = sz_ref[...]
    plane = sy + sz
    for k in range(share_x):
        inv_ref[k] = 1.0 / (sx_ref[row * share_x + k] + plane)
    weights = w_ref[me]
    for k, out in enumerate(y_products(r_ref, h_ref[me])):
        high, low = split(out)
        c = dot(jnp.concatenate([high, high, low], axis=1), weights)
        pad = c.shape[1] // (parts * fields)
        for part in range(parts):
            for f in range(fields):
                at = (part * fields + f) * pad
                o_ref[f, part * k_lo + k] = c[:, at : at + nz]


def z_kernel(cols, *refs):
    p_refs = refs[: cols - 1]
    acc_ref, inv_ref, w_ref, o_ref = refs[cols - 1 :]
    me = lax.axis_index("col")
    fields, share_x, share_y, nz = o_ref.shape
    k_lo = p_refs[0].shape[0]
    parts = share_x // k_lo
    for k in range(k_lo):
        c = None
        for step, p_ref in enumerate(p_refs, 1):
            source = lax.rem(me + cols - step, cols)
            high, low = split(p_ref[k])
            term = dot(jnp.concatenate([high, high, low], axis=1), w_ref[source])
            c = term if c is None else c + term
        pad = c.shape[1] // (parts * fields)
        for part in range(parts):
            for f in range(fields):
                at = (part * fields + f) * pad
                kx = part * k_lo + k
                o_ref[f, kx] = (acc_ref[f, kx] + c[:, at : at + nz]) * inv_ref[kx]


def call(kernel, out_shape, ins, outs, scratch=(), flops=0, bytes_accessed=0):
    return pl.pallas_call(
        kernel,
        out_shape=out_shape,
        in_specs=ins,
        out_specs=outs,
        scratch_shapes=scratch,
        compiler_params=pltpu.CompilerParams(vmem_limit_bytes=VMEM_GRANT),
        cost_estimate=pl.CostEstimate(
            flops=flops, bytes_accessed=bytes_accessed, transcendentals=0
        ),
    )


def f32(*shape):
    return jax.ShapeDtypeStruct(shape, jnp.float32)


def on_device(rows, cols, species, symbol_x, symbol_y, symbol_z):
    fields, nx, share_in, zs = species.shape
    ny, nz = share_in * rows, zs * cols
    share_x, share_y = nx // rows, ny // cols
    parts = LANES // (fields * zs)
    k_lo = share_x // parts
    assert parts * fields * zs == LANES and k_lo * parts == share_x
    assert share_in == SUBLANES

    hx = basis_table(nx).reshape(rows, parts, k_lo, nx).transpose(1, 0, 2, 3).reshape(nx, nx)
    high, low = split_table(hx)
    hx3 = jnp.asarray(np.concatenate([high, low, high], axis=1))
    high, low = split_table(basis_table(ny))
    hy3 = jnp.asarray(np.concatenate([high, low, high], axis=1).reshape(cols, share_y, 3 * ny))
    hz = basis_table(nz).reshape(cols, zs, nz)
    pad = -(-nz // LANES) * LANES
    wz = np.zeros((cols, parts * fields, zs, parts * fields, pad), np.float32)
    for j in range(parts * fields):
        wz[:, j, :, j, :nz] = hz
    wz = wz.reshape(cols, LANES, parts * fields * pad)
    high, low = split_table(wz)
    wz3 = jnp.asarray(np.concatenate([high, low, high], axis=1))

    send = call(
        x_kernel,
        f32(nx // parts * share_in, LANES),
        [VMEM, VMEM],
        VMEM,
        flops=6 * nx * nx * fields * share_in * zs,
        bytes_accessed=8 * species.size,
    )(jnp.transpose(species, (0, 2, 3, 1)), hx3)
    got = lax.all_to_all(
        send.reshape(rows, k_lo * share_in, LANES), "row", split_axis=0, concat_axis=0, tiled=True
    ).reshape(rows, k_lo, share_in, LANES)

    pieces = call(
        functools.partial(y_send_kernel, cols),
        [f32(k_lo, share_y, LANES)] * (cols - 1),
        [VMEM, VMEM],
        [VMEM] * (cols - 1),
        flops=6 * share_y * ny * k_lo * LANES * (cols - 1),
        bytes_accessed=8 * species.size,
    )(got, hy3)
    arrived = [
        lax.ppermute(piece, "col", [(d, (d + step) % cols) for d in range(cols)])
        for step, piece in enumerate(pieces, 1)
    ]
    kept, inverse = call(
        functools.partial(y_keep_kernel, cols),
        [f32(fields, share_x, share_y, nz), f32(share_x, share_y, nz)],
        [VMEM, VMEM, VMEM, SMEM, VMEM, VMEM],
        [VMEM, VMEM],
        scratch=[pltpu.VMEM((ny, LANES), jnp.float32)],
        flops=6 * share_y * ny * k_lo * LANES * 4,
        bytes_accessed=16 * species.size,
    )(got, hy3, wz3, symbol_x, symbol_y.reshape(1, ny), symbol_z.reshape(1, nz))
    return call(
        functools.partial(z_kernel, cols),
        f32(fields, share_x, share_y, nz),
        [VMEM] * (cols + 2),
        VMEM,
        flops=6 * share_y * share_x * fields * nz * nz,
        bytes_accessed=16 * species.size,
    )(*arrived, kept, inverse, wz3)


def solution(mesh):
    rows, cols = mesh.shape["row"], mesh.shape["col"]
    in_specs = (P(None, None, "row", "col"), P(), P(), P())
    out_specs = P(None, "row", "col", None)
    return jax.shard_map(
        functools.partial(on_device, rows, cols),
        mesh=mesh,
        in_specs=in_specs,
        out_specs=out_specs,
        check_vma=False,
    )
```

time: 40.2 us -> 26.7 us (0.66)
  blocking collectives: 0 us -> 17.3 us
  waiting for transfers between devices: 13.8 us -> 2.05 us
  starting transfers between devices: 11 us -> 1.59 us
  local copies, waits for them, and re-layouts: 7.65 us -> 2.53 us
  matrix products: 4.44 us -> 0 us
  Pallas kernels: 0 us -> 2.94 us
  other arithmetic: 2.88 us -> 0 us
    all_to_all x0 -> x1, blocking collectives: none -> 17.3 us  [on_device(): lax.all_to_all(send.reshape(rows, k_lo * share_in, LANES), 'row', split_a...]
    all_to_all x2 -> x0, waiting for transfers between devices: 13.8 us -> none  [the longest x1 8.47 us: on_device(): lax.all_to_all(part_values, 'row', split_axis=1, concat_axis=2, tiled=True)]
    all_to_all x2 -> x0, starting transfers between devices: 11 us -> none  [the longest x1 7.39 us: on_device(): lax.all_to_all(part_values, 'row', split_axis=1, concat_axis=2, tiled=True)]
    dot_general x2 -> x0, matrix products: 3.76 us -> none  [to_modes(): jnp.tensordot(values, basis_table(values.shape[dim]), axes=([dim], [0]),...]
    pallas_call x0 -> x4, Pallas kernels: none -> 2.94 us  [the longest x1 1.21 us: on_device(): call(functools.partial(z_kernel, cols), f32(fields, share_x, share_y, nz)...]
    unnamed x12 -> x14, local copies, waits for them, and re-layouts: 5.37 us -> 2.53 us
    all_to_all x2 -> x0, other arithmetic: 2.67 us -> none  [the longest x1 1.43 us: on_device(): lax.all_to_all(local_values, 'col', split_axis=2, concat_axis=3, tiled=True)]
    ppermute x0 -> x1, waiting for transfers between devices: none -> 2.05 us  [on_device(): lax.ppermute(piece, 'col', [(d, (d + step) % cols) for d in range(cols)])]
  transfers between devices with their start and end apart: 2 -> 1, of which waited for: 2 -> 1; matrix products, arithmetic and copies ran while one was open for 1% -> 0% of each run, Pallas kernels for 0% -> 4%
where the time goes in v1:
time: 26.7 us; the launch traced here: 26.5 us
  blocking collectives  17.3 us (65%)
  Pallas kernels  2.94 us (11%)
  local copies, waits for them, and re-layouts  2.53 us (9%)
  waiting for transfers between devices  2.05 us (8%)
  starting transfers between devices  1.59 us (6%)
    all_to_all x1, blocking collectives, on_device(): lax.all_to_all(send.reshape(rows, k_lo * share_in, LANES), 'row', split_a...  17.3 us
    unnamed x14, local copies, waits for them, and re-layouts  2.53 us
    ppermute x1, waiting for transfers between devices, on_device(): lax.ppermute(piece, 'col', [(d, (d + step) % cols) for d in range(cols)])  2.05 us
    ppermute x1, starting transfers between devices, on_device(): lax.ppermute(piece, 'col', [(d, (d + step) % cols) for d in range(cols)])  1.59 us
    pallas_call x1, Pallas kernels, on_device(): call(functools.partial(z_kernel, cols), f32(fields, share_x, share_y, nz)...  1.21 us
    pallas_call x1, Pallas kernels, on_device(): call(functools.partial(y_keep_kernel, cols), [f32(fields, share_x, share_...  1.05 us
  transfers between devices with their start and end apart: 1, of which 1 were waited for; matrix products, arithmetic and copies ran while one was open for 0% of the time, Pallas kernels for 4%

profile of v1, /device:TPU:0, one launch (start us, length us, event | category | flops | bytes accessed | tf_op | source)
XLA Modules:
  0.0 26.5 jit_solution(11193466653297375144)
XLA Ops:
  0.0 0.0 copy-start.2
  0.0 0.9 %copy-done.2 = f32[2,128,8,32]{1,3,2,0:T(8,128)S(1)} copy-done((f32[2,128,8,32]{1,3,2,0:T(8,128)S(1)}, f32[2,128,8,32]{1,3,2,0:T(8,128)}, u32[]{:S(2)}) %copy-start.2) | copy-done | bytes 262168
  1.0 0.0 copy-start.3
  1.0 0.9 %copy-done.3 = bf16[128,384]{1,0:T(8,128)(2,1)S(1)} copy-done((bf16[128,384]{1,0:T(8,128)(2,1)S(1)}, bf16[128,384]{1,0:T(8,128)(2,1)}, u32[]{:S(2)}) %copy-start.3) | copy-done | bytes 98328
  1.8 0.0 copy-start
  1.8 0.5 %shard_map.73 = f32[512,128]{1,0:T(8,128)S(1)} custom-call(f32[2,8,32,128]{3,2,1,0:T(8,128)S(1)} %bitcast.8, bf16[128,384]{1,0:T(8,128)(2,1)S(1)} %copy-done.3), custom_call_target="tpu_custom_call" | custom-call | flops 50331648 | bytes 524288 | tf_op jit(solution)/shard_map/pallas_call | solution.py:172
  2.3 0.0 copy-start.1
  2.3 17.3 %all_to_all.5 = f32[16,32,128]{2,1,0:T(8,128)S(1)} all-to-all(f32[16,32,128]{2,1,0:T(8,128)S(1)} %bitcast.7), channel_id=1, replica_groups=mesh['row'=16,'col'=2] {'row'}, dimensions={0} | all-to-all | bytes 524288 | tf_op jit(solution)/shard_map/all_to_all | solution.py:180
  19.7 0.0 copy-done.1
  19.7 0.2 shard_map.74
  19.9 1.6 %collective-permute-start = (f32[4,64,128]{2,1,0:T(8,128)S(1)}, f32[4,64,128]{2,1,0:T(8,128)S(1)}, u32[]{:S(2)}, u32[]{:S(2)}) collective-permute-start(f32[4,64,128]{2,1,0:T(8,128)S(1)} %shard_map.74), channel_id=1, source_target_pairs={{0,1},{1,0},{2,3},{3,2},{4,5},{5,4},{6,7},{7,6},{8,9},{9,8},{10,11... | collective-permute-start | bytes 393224 | tf_op jit(solution)/shard_map/ppermute | solution.py:193
  21.5 0.0 copy-start.4
  21.5 0.0 copy-start.5
  21.5 0.0 copy-start.6
  21.5 0.0 copy-done
  21.5 0.6 %copy-done.4 = f32[128]{0:T(128)S(1)} copy-done((f32[128]{0:T(128)S(1)}, f32[128]{0:T(128)}, u32[]{:S(2)}) %copy-start.4) | copy-done | bytes 536
  22.1 0.0 copy-done.5
  22.1 0.0 copy-done.6
  22.2 1.0 %shard_map.75 = (f32[2,8,64,64]{3,2,1,0:T(8,128)S(1)}, f32[8,64,64]{2,1,0:T(8,128)S(1)}) custom-call(f32[16,4,8,128]{3,2,1,0:T(8,128)S(1)} %bitcast.6, bf16[2,64,384]{2,1,0:T(8,128)(2,1)S(1)} %copy-done.1, bf16[2,384,512]{2,1,0:T(8,128)(2,1)S(1)} %copy-done, f32[128]{0:T(128)S(1)} %copy-done.4, f32[1,128]{1,0:T(1,128)S(1)} %bitcast.9, f32[1,64]{1,0:T(1,128)S(1)} %bitcast.10), custom_call_target="tpu_custom_call" | custom-call | flops 100663296 | bytes 1048576 | tf_op jit(solution)/shard_map/pallas_call | solution.py:196
  23.2 2.1 %collective-permute-done.refs_0_ = f32[4,64,128]{2,1,0:T(8,128)S(1)} collective-permute-done((f32[4,64,128]{2,1,0:T(8,128)S(1)}, f32[4,64,128]{2,1,0:T(8,128)S(1)}, u32[]{:S(2)}, u32[]{:S(2)}) %collective-permute-start) | collective-permute-done | bytes 131104 | tf_op jit(solution)/shard_map/ppermute | solution.py:193
  25.3 1.2 %shard_map.76 = f32[2,8,64,64]{3,2,1,0:T(8,128)} custom-call(f32[4,64,128]{2,1,0:T(8,128)S(1)} %collective-permute-done.refs_0_, f32[2,8,64,64]{3,2,1,0:T(8,128)S(1)} %get-tuple-element.7.refs_1_, f32[8,64,64]{2,1,0:T(8,128)S(1)} %get-tuple-element.8.refs_2_, bf16[2,384,512]{2,1,0:T(8,128)(2,1)S(1)} %copy-done), custom_call_target="tpu_custom_call" | custom-call | flops 25165824 | bytes 1048576 | tf_op jit(solution)/shard_map/pallas_call | solution.py:205
Async XLA Ops:
  0.0 0.9 %copy-start.2 = (f32[2,128,8,32]{1,3,2,0:T(8,128)S(1)}, f32[2,128,8,32]{1,3,2,0:T(8,128)}, u32[]{:S(2)}) copy-start(f32[2,128,8,32]{1,3,2,0:T(8,128)} %param.7) | copy-start | bytes 786436
  1.0 0.9 %copy-start.3 = (bf16[128,384]{1,0:T(8,128)(2,1)S(1)}, bf16[128,384]{1,0:T(8,128)(2,1)}, u32[]{:S(2)}) copy-start(bf16[128,384]{1,0:T(8,128)(2,1)} %constant.6.clone.h_ref) | copy-start | bytes 294916
  1.8 19.6 %copy-start = (bf16[2,384,512]{2,1,0:T(8,128)(2,1)S(1)}, bf16[2,384,512]{2,1,0:T(8,128)(2,1)}, u32[]{:S(2)}) copy-start(bf16[2,384,512]{2,1,0:T(8,128)(2,1)} %constant.8.clone.w_ref.refs_3_) | copy-start | bytes 2359300
  2.3 17.3 %copy-start.1 = (bf16[2,64,384]{2,1,0:T(8,128)(2,1)S(1)}, bf16[2,64,384]{2,1,0:T(8,128)(2,1)}, u32[]{:S(2)}) copy-start(bf16[2,64,384]{2,1,0:T(8,128)(2,1)} %constant.7.clone.h_ref) | copy-start | bytes 294916
  19.9 5.4 %collective-permute-start = (f32[4,64,128]{2,1,0:T(8,128)S(1)}, f32[4,64,128]{2,1,0:T(8,128)S(1)}, u32[]{:S(2)}, u32[]{:S(2)}) collective-permute-start(f32[4,64,128]{2,1,0:T(8,128)S(1)} %shard_map.74), channel_id=1, source_target_pairs={{0,1},{1,0},{2,3},{3,2},{4,5},{5,4},{6,7},{7,6},{8,9},{9,8},{10,11... | collective-permute-start | bytes 393224 | tf_op jit(solution)/shard_map/ppermute | solution.py:193
  21.5 0.7 %copy-start.4 = (f32[128]{0:T(128)S(1)}, f32[128]{0:T(128)}, u32[]{:S(2)}) copy-start(f32[128]{0:T(128)} %sx_ref.1) | copy-start | bytes 1540
  21.5 0.7 %copy-start.5 = (f32[128]{0:T(128)S(1)}, f32[128]{0:T(128)}, u32[]{:S(2)}) copy-start(f32[128]{0:T(128)} %param.9) | copy-start | bytes 1540
  21.5 0.7 %copy-start.6 = (f32[64]{0:T(128)S(1)}, f32[64]{0:T(128)}, u32[]{:S(2)}) copy-start(f32[64]{0:T(128)} %param.10) | copy-start | bytes 772

commit v2 on v1

v2 whole, which is shorter than its diff:
```python
import functools

import jax
import jax.numpy as jnp
import numpy as np
from jax import lax
from jax.experimental import pallas as pl
from jax.experimental.pallas import tpu as pltpu
from jax.sharding import PartitionSpec as P

LANES = 128
SUBLANES = 8
VMEM_GRANT = 12 * 2**20
Y_STEP = 2
GROUPS = 2
VMEM = pl.BlockSpec(memory_space=pltpu.VMEM)
SMEM = pl.BlockSpec(memory_space=pltpu.SMEM)
HBM = pl.BlockSpec(memory_space=pltpu.HBM)


def basis_table(count):
    rank = np.arange(count)
    odd = 2 * rank + 1
    angle = np.pi / (4 * count) * (odd[:, None] * odd[None, :] % (8 * count))
    return (np.cos(angle) * (2.0 / count) ** 0.5).astype(np.float32)


def split_table(table):
    high = table.astype(jnp.bfloat16)
    low = (table - high.astype(np.float32)).astype(jnp.bfloat16)
    return high, low


def split(values):
    high = values.astype(jnp.bfloat16)
    low = (values - high.astype(jnp.float32)).astype(jnp.bfloat16)
    return high, low


def dot(left, right):
    return jnp.dot(left, right, preferred_element_type=jnp.float32)


def dot_nt(left, right):
    return lax.dot_general(
        left, right, (((1,), (1,)), ((), ())), preferred_element_type=jnp.float32
    )


def x_kernel(a_hbm, h_hbm, o_ref, a_ref, h_ref, a_sems, h_sem):
    fields, ys, zs, nx = a_ref.shape
    half = fields * zs
    parts = LANES // half
    rows = h_ref.shape[0] // parts
    table_copy = pltpu.make_async_copy(h_hbm, h_ref, h_sem)
    table_copy.start()
    copies = []
    for i in range(0, ys, Y_STEP):
        at = (slice(None), pl.ds(i, Y_STEP))
        copies.append(pltpu.make_async_copy(a_hbm.at[at], a_ref.at[at], a_sems.at[i // Y_STEP]))
        copies[-1].start()
    table_copy.wait()
    table = jnp.concatenate([h_ref[...], h_ref[:, :nx]], axis=1)
    lane = lax.broadcasted_iota(jnp.int32, (rows, LANES), 1)
    for i in range(0, ys, Y_STEP):
        copies[i // Y_STEP].wait()
        a = [a_ref[f, y] for y in range(i, i + Y_STEP) for _ in range(parts) for f in range(fields)]
        high, low = split(jnp.concatenate(a, axis=0))
        c = dot_nt(table, jnp.concatenate([high, high, low], axis=1))
        for j in range(Y_STEP):
            mine = c[:, j * LANES : (j + 1) * LANES]
            out = mine[:rows]
            for part in range(1, parts):
                out = jnp.where(lane < part * half, out, mine[part * rows : (part + 1) * rows])
            o_ref[pl.ds(i + j, rows, stride=ys), :] = out


def y_products(r_ref, h_ref, target, ks):
    count, _, ys, lanes = r_ref.shape
    table = h_ref[target]
    table = jnp.concatenate([table, table[:, : count * ys]], axis=1)
    outs = []
    for k in ks:
        high, low = split(r_ref[:, k].reshape(count * ys, lanes))
        outs.append(dot(table, jnp.concatenate([high, high, low], axis=0)))
    return outs


def y_send_kernel(cols, ks, r_ref, h_ref, *o_refs):
    me = lax.axis_index("col")
    for step, o_ref in enumerate(o_refs, 1):
        target = lax.rem(me + step, cols)
        for i, out in enumerate(y_products(r_ref, h_ref, target, ks)):
            o_ref[i] = out


def z_products(p, weights):
    high, low = split(p)
    return dot(jnp.concatenate([high, high, low], axis=1), weights)


def y_keep_kernel(cols, r_ref, h_ref, w_ref, sx_ref, sy_ref, sz_ref, o_ref, inv_ref, sy_scr):
    me = lax.axis_index("col")
    row = lax.axis_index("row")
    fields, share_x, share_y, nz = o_ref.shape
    k_lo = r_ref.shape[1]
    parts = share_x // k_lo
    ny = sy_ref.shape[1]
    for i in range(ny // LANES):
        sy_scr[i * LANES : (i + 1) * LANES, :] = jnp.broadcast_to(
            sy_ref[:, i * LANES : (i + 1) * LANES], (LANES, LANES)
        ).T
    sy = sy_scr[pl.ds(me * share_y, share_y), :][:, :1]
    plane = sy + sz_ref[...]
    for k in range(share_x):
        inv_ref[k] = 1.0 / (sx_ref[row * share_x + k] + plane)
    weights = w_ref[me]
    for k, out in enumerate(y_products(r_ref, h_ref, me, range(k_lo))):
        c = z_products(out, weights)
        pad = c.shape[1] // (parts * fields)
        for part in range(parts):
            for f in range(fields):
                at = (part * fields + f) * pad
                o_ref[f, part * k_lo + k] = c[:, at : at + nz]


def z_kernel(cols, k_lo, ks, *refs):
    p_refs = refs[: cols - 1]
    acc_ref, inv_ref, w_ref = refs[cols - 1 : cols + 2]
    o_hbm, o_ref, sems = refs[-3:]
    me = lax.axis_index("col")
    fields, share_x, share_y, nz = acc_ref.shape
    parts = share_x // k_lo
    copies = []
    for i, k in enumerate(ks):
        c = None
        for step, p_ref in enumerate(p_refs, 1):
            source = lax.rem(me + cols - step, cols)
            term = z_products(p_ref[i], w_ref[source])
            c = term if c is None else c + term
        pad = c.shape[1] // (parts * fields)
        for part in range(parts):
            for f in range(fields):
                at = (part * fields + f) * pad
                kx = part * k_lo + k
                slot = (i * parts + part) * fields + f
                o_ref[slot] = (acc_ref[f, kx] + c[:, at : at + nz]) * inv_ref[kx]
                copies.append(
                    pltpu.make_async_copy(o_ref.at[slot], o_hbm.at[f, kx], sems.at[slot])
                )
                copies[-1].start()
    for copy in copies:
        copy.wait()


def call(kernel, out_shape, ins, outs, scratch=(), flops=0, bytes_accessed=0, aliases=None):
    return pl.pallas_call(
        kernel,
        out_shape=out_shape,
        in_specs=ins,
        out_specs=outs,
        scratch_shapes=scratch,
        input_output_aliases=aliases or {},
        compiler_params=pltpu.CompilerParams(vmem_limit_bytes=VMEM_GRANT),
        cost_estimate=pl.CostEstimate(
            flops=flops, bytes_accessed=bytes_accessed, transcendentals=0
        ),
    )


def f32(*shape):
    return jax.ShapeDtypeStruct(shape, jnp.float32)


def on_device(rows, cols, species, symbol_x, symbol_y, symbol_z):
    fields, nx, share_in, zs = species.shape
    ny, nz = share_in * rows, zs * cols
    share_x, share_y = nx // rows, ny // cols
    parts = LANES // (fields * zs)
    k_lo = share_x // parts
    assert parts * fields * zs == LANES and k_lo * parts == share_x
    assert share_in == SUBLANES

    hx = basis_table(nx).reshape(rows, parts, k_lo, nx).transpose(1, 0, 2, 3).reshape(nx, nx)
    high, low = split_table(hx)
    hx2 = jnp.asarray(np.concatenate([high, low], axis=1))
    high, low = split_table(basis_table(ny))
    hy2 = jnp.asarray(np.concatenate([high, low], axis=1).reshape(cols, share_y, 2 * ny))
    hz = basis_table(nz).reshape(cols, zs, nz)
    pad = -(-nz // LANES) * LANES
    wz = np.zeros((cols, parts * fields, zs, parts * fields, pad), np.float32)
    for j in range(parts * fields):
        wz[:, j, :, j, :nz] = hz
    wz = wz.reshape(cols, LANES, parts * fields * pad)
    high, low = split_table(wz)
    wz3 = jnp.asarray(np.concatenate([high, low, high], axis=1))

    moved = jnp.transpose(species, (0, 2, 3, 1))
    send = call(
        x_kernel,
        f32(nx // parts * share_in, LANES),
        [HBM, HBM],
        VMEM,
        scratch=[
            pltpu.VMEM(moved.shape, jnp.float32),
            pltpu.VMEM(hx2.shape, jnp.bfloat16),
            pltpu.SemaphoreType.DMA((share_in // Y_STEP,)),
            pltpu.SemaphoreType.DMA,
        ],
        flops=6 * nx * nx * fields * share_in * zs,
        bytes_accessed=8 * species.size,
    )(pltpu.with_memory_space_constraint(moved, pltpu.HBM), pltpu.with_memory_space_constraint(hx2, pltpu.HBM))
    got = lax.all_to_all(
        send.reshape(rows, k_lo * share_in, LANES), "row", split_axis=0, concat_axis=0, tiled=True
    ).reshape(rows, k_lo, share_in, LANES)

    size = k_lo // GROUPS
    groups = [range(g * size, (g + 1) * size) for g in range(GROUPS)]
    arrived = []
    for ks in groups:
        pieces = call(
            functools.partial(y_send_kernel, cols, ks),
            [f32(size, share_y, LANES)] * (cols - 1),
            [VMEM, VMEM],
            [VMEM] * (cols - 1),
            flops=6 * share_y * ny * size * LANES * (cols - 1),
            bytes_accessed=8 * species.size // GROUPS,
        )(got, hy2)
        arrived.append(
            [
                lax.ppermute(piece, "col", [(d, (d + step) % cols) for d in range(cols)])
                for step, piece in enumerate(pieces, 1)
            ]
        )
    kept, inverse = call(
        functools.partial(y_keep_kernel, cols),
        [f32(fields, share_x, share_y, nz), f32(share_x, share_y, nz)],
        [VMEM, VMEM, VMEM, SMEM, VMEM, VMEM],
        [VMEM, VMEM],
        scratch=[pltpu.VMEM((ny, LANES), jnp.float32)],
        flops=6 * share_y * ny * k_lo * LANES * 4,
        bytes_accessed=16 * species.size,
    )(got, hy2, wz3, symbol_x, symbol_y.reshape(1, ny), symbol_z.reshape(1, nz))
    out = None
    slots = size * parts * fields
    for ks, parts_in in zip(groups, arrived):
        args = [*parts_in, kept, inverse, wz3] + ([] if out is None else [out])
        out = call(
            functools.partial(z_kernel, cols, k_lo, ks),
            f32(fields, share_x, share_y, nz),
            [VMEM] * (cols + 2) + ([] if out is None else [HBM]),
            HBM,
            scratch=[
                pltpu.VMEM((slots, share_y, nz), jnp.float32),
                pltpu.SemaphoreType.DMA((slots,)),
            ],
            flops=6 * share_y * share_x * fields * nz * nz // GROUPS,
            bytes_accessed=16 * species.size // GROUPS,
            aliases={} if out is None else {cols + 2: 0},
        )(*args)
    return out


def solution(mesh):
    rows, cols = mesh.shape["row"], mesh.shape["col"]
    in_specs = (P(None, None, "row", "col"), P(), P(), P())
    out_specs = P(None, "row", "col", None)
    return jax.shard_map(
        functools.partial(on_device, rows, cols),
        mesh=mesh,
        in_specs=in_specs,
        out_specs=out_specs,
        check_vma=False,
    )
```

time: 26.7 us -> 26.9 us (level)
  Pallas kernels: 2.94 us -> 5.38 us
  local copies, waits for them, and re-layouts: 2.53 us -> 0.69 us
  waiting for transfers between devices: 2.05 us -> 1.03 us
  starting transfers between devices: 1.59 us -> 2.16 us
    pallas_call x3 -> x5, Pallas kernels: 1.89 us -> 4.33 us  [the longest x1 2.02 us: on_device(): call(x_kernel, f32(nx // parts * share_in, LANES), [HBM, HBM], VMEM, scra...]
    unnamed x14 -> x10, local copies, waits for them, and re-layouts: 2.53 us -> 0.69 us
    ppermute x1 -> x2, waiting for transfers between devices: 2.05 us -> 1.03 us  [on_device(): lax.ppermute(piece, 'col', [(d, (d + step) % cols) for d in range(cols)])]
    ppermute x1 -> x2, starting transfers between devices: 1.59 us -> 2.16 us  [on_device(): lax.ppermute(piece, 'col', [(d, (d + step) % cols) for d in range(cols)])]
  transfers between devices with their start and end apart: 1 -> 2, of which waited for: 1 -> 2; matrix products, arithmetic and copies ran while one was open for 0% -> 0% of each run, Pallas kernels for 4% -> 8%
where the time goes in v2:
time: 26.9 us; the launch traced here: 26.6 us
  blocking collectives  17.3 us (64%)
  Pallas kernels  5.38 us (20%)
  starting transfers between devices  2.16 us (8%)
  waiting for transfers between devices  1.03 us (4%)
  local copies, waits for them, and re-layouts  0.69 us (3%)
    all_to_all x1, blocking collectives, on_device(): lax.all_to_all(send.reshape(rows, k_lo * share_in, LANES), 'row', split_a...  17.3 us
    ppermute x2, starting transfers between devices, on_device(): lax.ppermute(piece, 'col', [(d, (d + step) % cols) for d in range(cols)])  2.16 us
    pallas_call x1, Pallas kernels, on_device(): call(x_kernel, f32(nx // parts * share_in, LANES), [HBM, HBM], VMEM, scra...  2.02 us
    pallas_call x2, Pallas kernels, on_device(): call(functools.partial(z_kernel, cols, k_lo, ks), f32(fields, share_x, sh...  1.97 us
    pallas_call x1, Pallas kernels, on_device(): call(functools.partial(y_keep_kernel, cols), [f32(fields, share_x, share_...  1.05 us
    ppermute x2, waiting for transfers between devices, on_device(): lax.ppermute(piece, 'col', [(d, (d + step) % cols) for d in range(cols)])  1.03 us
    unnamed x10, local copies, waits for them, and re-layouts  0.69 us
  transfers between devices with their start and end apart: 2, of which 2 were waited for; matrix products, arithmetic and copies ran while one was open for 0% of the time, Pallas kernels for 8%

profile of v2, /device:TPU:0, one launch (start us, length us, event | category | flops | bytes accessed | tf_op | source)
XLA Modules:
  0.0 26.6 jit_solution(17631223486218394569)
XLA Ops:
  0.0 0.0 copy-start.1
  0.0 2.0 %shard_map.73 = f32[512,128]{1,0:T(8,128)S(1)} custom-call(f32[2,8,32,128]{3,2,1,0:T(8,128)} %bitcast.11, bf16[128,256]{1,0:T(8,128)(2,1)} %constant.6.clone.h_hbm), custom_call_target="tpu_custom_call" | custom-call | flops 50331648 | bytes 524288 | tf_op jit(solution)/shard_map/pallas_call | solution.py:199
  2.0 0.0 copy-start
  2.0 17.3 %all_to_all.5 = f32[16,32,128]{2,1,0:T(8,128)S(1)} all-to-all(f32[16,32,128]{2,1,0:T(8,128)S(1)} %bitcast.8), channel_id=1, replica_groups=mesh['row'=16,'col'=2] {'row'}, dimensions={0} | all-to-all | bytes 524288 | tf_op jit(solution)/shard_map/all_to_all | solution.py:213
  19.4 0.0 copy-done.1
  19.4 0.2 shard_map.76
  19.6 1.6 %collective-permute-start.1 = (f32[2,64,128]{2,1,0:T(8,128)S(1)}, f32[2,64,128]{2,1,0:T(8,128)S(1)}, u32[]{:S(2)}, u32[]{:S(2)}) collective-permute-start(f32[2,64,128]{2,1,0:T(8,128)S(1)} %shard_map.76), channel_id=1, source_target_pairs={{0,1},{1,0},{2,3},{3,2},{4,5},{5,4},{6,7},{7,6},{8,9},{9,8},{10,11... | collective-permute-start | bytes 196616 | tf_op jit(solution)/shard_map/ppermute | solution.py:231
  21.1 0.2 shard_map.74
  21.3 0.6 %collective-permute-start = (f32[2,64,128]{2,1,0:T(8,128)S(1)}, f32[2,64,128]{2,1,0:T(8,128)S(1)}, u32[]{:S(2)}, u32[]{:S(2)}) collective-permute-start(f32[2,64,128]{2,1,0:T(8,128)S(1)} %shard_map.74), channel_id=1, source_target_pairs={{0,1},{1,0},{2,3},{3,2},{4,5},{5,4},{6,7},{7,6},{8,9},{9,8},{10,11... | collective-permute-start | bytes 196616 | tf_op jit(solution)/shard_map/ppermute | solution.py:231
  21.9 0.0 copy-start.2
  21.9 0.0 copy-start.3
  21.9 0.0 copy-start.4
  21.9 0.0 copy-done
  21.9 0.6 %copy-done.2 = f32[128]{0:T(128)S(1)} copy-done((f32[128]{0:T(128)S(1)}, f32[128]{0:T(128)}, u32[]{:S(2)}) %copy-start.2) | copy-done | bytes 536
  22.6 0.0 copy-done.3
  22.6 0.0 copy-done.4
  22.6 1.0 %shard_map.75 = (f32[2,8,64,64]{3,2,1,0:T(8,128)S(1)}, f32[8,64,64]{2,1,0:T(8,128)S(1)}) custom-call(f32[16,4,8,128]{3,2,1,0:T(8,128)S(1)} %bitcast.7, bf16[2,64,256]{2,1,0:T(8,128)(2,1)S(1)} %copy-done.1, bf16[2,384,512]{2,1,0:T(8,128)(2,1)S(1)} %copy-done, f32[128]{0:T(128)S(1)} %copy-done.2, f32[1,128]{1,0:T(1,128)S(1)} %bitcast.9, f32[1,64]{1,0:T(1,128)S(1)} %bitcast.10), custom_call_target="tpu_custom_call" | custom-call | flops 100663296 | bytes 1048576 | tf_op jit(solution)/shard_map/pallas_call | solution.py:235
  23.6 0.5 %collective-permute-done.1.refs_0_ = f32[2,64,128]{2,1,0:T(8,128)S(1)} collective-permute-done((f32[2,64,128]{2,1,0:T(8,128)S(1)}, f32[2,64,128]{2,1,0:T(8,128)S(1)}, u32[]{:S(2)}, u32[]{:S(2)}) %collective-permute-start.1) | collective-permute-done | bytes 65568 | tf_op jit(solution)/shard_map/ppermute | solution.py:231
  24.2 1.0 %shard_map.77.refs_4_ = f32[2,8,64,64]{3,2,1,0:T(8,128)} custom-call(f32[2,64,128]{2,1,0:T(8,128)S(1)} %collective-permute-done.1.refs_0_, f32[2,8,64,64]{3,2,1,0:T(8,128)S(1)} %get-tuple-element.7.refs_1_, f32[8,64,64]{2,1,0:T(8,128)S(1)} %get-tuple-element.8.refs_2_, bf16[2,384,512]{2,1,0:T(8,128)(2,1)S(1)} %copy-done), custom_call_target="tpu_custom_call" | custom-call | flops 12582912 | bytes 524288 | tf_op jit(solution)/shard_map/pallas_call | solution.py:248
  25.2 0.5 %collective-permute-done.refs_0_ = f32[2,64,128]{2,1,0:T(8,128)S(1)} collective-permute-done((f32[2,64,128]{2,1,0:T(8,128)S(1)}, f32[2,64,128]{2,1,0:T(8,128)S(1)}, u32[]{:S(2)}, u32[]{:S(2)}) %collective-permute-start) | collective-permute-done | bytes 65568 | tf_op jit(solution)/shard_map/ppermute | solution.py:231
  25.7 1.0 %shard_map.78 = f32[2,8,64,64]{3,2,1,0:T(8,128)} custom-call(f32[2,64,128]{2,1,0:T(8,128)S(1)} %collective-permute-done.refs_0_, f32[2,8,64,64]{3,2,1,0:T(8,128)S(1)} %get-tuple-element.7.refs_1_, f32[8,64,64]{2,1,0:T(8,128)S(1)} %get-tuple-element.8.refs_2_, bf16[2,384,512]{2,1,0:T(8,128)(2,1)S(1)} %copy-done, ...), custom_call_target="tpu_custom_call", output_to_operand_aliasing={{}: (4, {})} | custom-call | flops 12582912 | bytes 524288 | tf_op jit(solution)/shard_map/pallas_call | solution.py:248
Async XLA Ops:
  0.0 19.4 %copy-start.1 = (bf16[2,64,256]{2,1,0:T(8,128)(2,1)S(1)}, bf16[2,64,256]{2,1,0:T(8,128)(2,1)}, u32[]{:S(2)}) copy-start(bf16[2,64,256]{2,1,0:T(8,128)(2,1)} %constant.7.clone.h_ref) | copy-start | bytes 196612
  2.0 19.9 %copy-start = (bf16[2,384,512]{2,1,0:T(8,128)(2,1)S(1)}, bf16[2,384,512]{2,1,0:T(8,128)(2,1)}, u32[]{:S(2)}) copy-start(bf16[2,384,512]{2,1,0:T(8,128)(2,1)} %constant.8.clone.w_ref.refs_3_) | copy-start | bytes 2359300
  19.6 4.6 %collective-permute-start.1 = (f32[2,64,128]{2,1,0:T(8,128)S(1)}, f32[2,64,128]{2,1,0:T(8,128)S(1)}, u32[]{:S(2)}, u32[]{:S(2)}) collective-permute-start(f32[2,64,128]{2,1,0:T(8,128)S(1)} %shard_map.76), channel_id=1, source_target_pairs={{0,1},{1,0},{2,3},{3,2},{4,5},{5,4},{6,7},{7,6},{8,9},{9,8},{10,11... | collective-permute-start | bytes 196616 | tf_op jit(solution)/shard_map/ppermute | solution.py:231
  21.3 4.3 %collective-permute-start = (f32[2,64,128]{2,1,0:T(8,128)S(1)}, f32[2,64,128]{2,1,0:T(8,128)S(1)}, u32[]{:S(2)}, u32[]{:S(2)}) collective-permute-start(f32[2,64,128]{2,1,0:T(8,128)S(1)} %shard_map.74), channel_id=1, source_target_pairs={{0,1},{1,0},{2,3},{3,2},{4,5},{5,4},{6,7},{7,6},{8,9},{9,8},{10,11... | collective-permute-start | bytes 196616 | tf_op jit(solution)/shard_map/ppermute | solution.py:231
  21.9 0.7 %copy-start.2 = (f32[128]{0:T(128)S(1)}, f32[128]{0:T(128)}, u32[]{:S(2)}) copy-start(f32[128]{0:T(128)} %sx_ref.1) | copy-start | bytes 1540
  21.9 0.7 %copy-start.3 = (f32[128]{0:T(128)S(1)}, f32[128]{0:T(128)}, u32[]{:S(2)}) copy-start(f32[128]{0:T(128)} %param.9) | copy-start | bytes 1540
  21.9 0.7 %copy-start.4 = (f32[64]{0:T(128)S(1)}, f32[64]{0:T(128)}, u32[]{:S(2)}) copy-start(f32[64]{0:T(128)} %param.10) | copy-start | bytes 772

commit v3 on v2

--- a/solution.py
+++ b/solution.py
@@ -12,7 +12,7 @@
 SUBLANES = 8
 VMEM_GRANT = 12 * 2**20
 Y_STEP = 2
-GROUPS = 2
+GROUPS = 1
 VMEM = pl.BlockSpec(memory_space=pltpu.VMEM)
 SMEM = pl.BlockSpec(memory_space=pltpu.SMEM)
 HBM = pl.BlockSpec(memory_space=pltpu.HBM)
@@ -47,23 +47,22 @@
     )
 
 
-def x_kernel(a_hbm, h_hbm, o_ref, a_ref, h_ref, a_sems, h_sem):
+def x_kernel(a_hbm, h_hbm, o_ref, a_ref, h_ref, a_sem, h_sem):
     fields, ys, zs, nx = a_ref.shape
     half = fields * zs
     parts = LANES // half
     rows = h_ref.shape[0] // parts
-    table_copy = pltpu.make_async_copy(h_hbm, h_ref, h_sem)
-    table_copy.start()
-    copies = []
-    for i in range(0, ys, Y_STEP):
-        at = (slice(None), pl.ds(i, Y_STEP))
-        copies.append(pltpu.make_async_copy(a_hbm.at[at], a_ref.at[at], a_sems.at[i // Y_STEP]))
-        copies[-1].start()
-    table_copy.wait()
+    copies = [
+        pltpu.make_async_copy(h_hbm, h_ref, h_sem),
+        pltpu.make_async_copy(a_hbm, a_ref, a_sem),
+    ]
+    for copy in copies:
+        copy.start()
+    for copy in copies:
+        copy.wait()
     table = jnp.concatenate([h_ref[...], h_ref[:, :nx]], axis=1)
     lane = lax.broadcasted_iota(jnp.int32, (rows, LANES), 1)
     for i in range(0, ys, Y_STEP):
-        copies[i // Y_STEP].wait()
         a = [a_ref[f, y] for y in range(i, i + Y_STEP) for _ in range(parts) for f in range(fields)]
         high, low = split(jnp.concatenate(a, axis=0))
         c = dot_nt(table, jnp.concatenate([high, high, low], axis=1))
@@ -204,7 +203,7 @@
         scratch=[
             pltpu.VMEM(moved.shape, jnp.float32),
             pltpu.VMEM(hx2.shape, jnp.bfloat16),
-            pltpu.SemaphoreType.DMA((share_in // Y_STEP,)),
+            pltpu.SemaphoreType.DMA,
             pltpu.SemaphoreType.DMA,
         ],
         flops=6 * nx * nx * fields * share_in * zs,

time: 26.9 us -> 25.8 us (0.959)
  Pallas kernels: 5.38 us -> 3.92 us
  waiting for transfers between devices: 1.03 us -> 2.06 us
  starting transfers between devices: 2.16 us -> 1.58 us
    ppermute x2 -> x1, waiting for transfers between devices: 1.03 us -> 2.06 us  [on_device(): lax.ppermute(piece, 'col', [(d, (d + step) % cols) for d in range(cols)])]
    pallas_call x2 -> x1, Pallas kernels: 1.97 us -> 1.19 us  [on_device(): call(functools.partial(z_kernel, cols, k_lo, ks), f32(fields, share_x, sh...]
    ppermute x2 -> x1, starting transfers between devices: 2.16 us -> 1.58 us  [on_device(): lax.ppermute(piece, 'col', [(d, (d + step) % cols) for d in range(cols)])]
    pallas_call x1, Pallas kernels: 2.02 us -> 1.46 us  [on_device(): call(x_kernel, f32(nx // parts * share_in, LANES), [HBM, HBM], VMEM, scra...]
  transfers between devices with their start and end apart: 2 -> 1, of which waited for: 2 -> 1; matrix products, arithmetic and copies ran while one was open for 0% -> 0% of each run, Pallas kernels for 8% -> 4%
where the time goes in v3:
time: 25.8 us; the launch traced here: 25.6 us
  blocking collectives  17.3 us (67%)
  Pallas kernels  3.92 us (15%)
  waiting for transfers between devices  2.06 us (8%)
  starting transfers between devices  1.58 us (6%)
  local copies, waits for them, and re-layouts  0.69 us (3%)
    all_to_all x1, blocking collectives, on_device(): lax.all_to_all(send.reshape(rows, k_lo * share_in, LANES), 'row', split_a...  17.3 us
    ppermute x1, waiting for transfers between devices, on_device(): lax.ppermute(piece, 'col', [(d, (d + step) % cols) for d in range(cols)])  2.06 us
    ppermute x1, starting transfers between devices, on_device(): lax.ppermute(piece, 'col', [(d, (d + step) % cols) for d in range(cols)])  1.58 us
    pallas_call x1, Pallas kernels, on_device(): call(x_kernel, f32(nx // parts * share_in, LANES), [HBM, HBM], VMEM, scra...  1.46 us
    pallas_call x1, Pallas kernels, on_device(): call(functools.partial(z_kernel, cols, k_lo, ks), f32(fields, share_x, sh...  1.19 us
    pallas_call x1, Pallas kernels, on_device(): call(functools.partial(y_keep_kernel, cols), [f32(fields, share_x, share_...  1.05 us
    unnamed x10, local copies, waits for them, and re-layouts  0.69 us
  transfers between devices with their start and end apart: 1, of which 1 were waited for; matrix products, arithmetic and copies ran while one was open for 0% of the time, Pallas kernels for 4%

profile of v3, /device:TPU:0, one launch (start us, length us, event | category | flops | bytes accessed | tf_op | source)
XLA Modules:
  0.0 25.6 jit_solution(7768644840996086652)
XLA Ops:
  0.0 0.0 copy-start
  0.0 1.5 %shard_map.73 = f32[512,128]{1,0:T(8,128)S(1)} custom-call(f32[2,8,32,128]{3,2,1,0:T(8,128)} %bitcast.10, bf16[128,256]{1,0:T(8,128)(2,1)} %constant.6.clone.h_hbm), custom_call_target="tpu_custom_call" | custom-call | flops 50331648 | bytes 524288 | tf_op jit(solution)/shard_map/pallas_call | solution.py:198
  1.5 0.0 copy-start.1
  1.5 17.3 %all_to_all.5 = f32[16,32,128]{2,1,0:T(8,128)S(1)} all-to-all(f32[16,32,128]{2,1,0:T(8,128)S(1)} %bitcast.7), channel_id=1, replica_groups=mesh['row'=16,'col'=2] {'row'}, dimensions={0} | all-to-all | bytes 524288 | tf_op jit(solution)/shard_map/all_to_all | solution.py:212
  18.8 0.0 copy-done.1
  18.8 0.2 shard_map.74
  19.0 1.6 %collective-permute-start = (f32[4,64,128]{2,1,0:T(8,128)S(1)}, f32[4,64,128]{2,1,0:T(8,128)S(1)}, u32[]{:S(2)}, u32[]{:S(2)}) collective-permute-start(f32[4,64,128]{2,1,0:T(8,128)S(1)} %shard_map.74), channel_id=1, source_target_pairs={{0,1},{1,0},{2,3},{3,2},{4,5},{5,4},{6,7},{7,6},{8,9},{9,8},{10,11... | collective-permute-start | bytes 393224 | tf_op jit(solution)/shard_map/ppermute | solution.py:230
  20.6 0.0 copy-start.2
  20.6 0.0 copy-start.3
  20.6 0.0 copy-start.4
  20.6 0.0 copy-done
  20.6 0.6 %copy-done.2 = f32[128]{0:T(128)S(1)} copy-done((f32[128]{0:T(128)S(1)}, f32[128]{0:T(128)}, u32[]{:S(2)}) %copy-start.2) | copy-done | bytes 536
  21.3 0.0 copy-done.3
  21.3 0.0 copy-done.4
  21.3 1.0 %shard_map.75 = (f32[2,8,64,64]{3,2,1,0:T(8,128)S(1)}, f32[8,64,64]{2,1,0:T(8,128)S(1)}) custom-call(f32[16,4,8,128]{3,2,1,0:T(8,128)S(1)} %bitcast.6, bf16[2,64,256]{2,1,0:T(8,128)(2,1)S(1)} %copy-done.1, bf16[2,384,512]{2,1,0:T(8,128)(2,1)S(1)} %copy-done, f32[128]{0:T(128)S(1)} %copy-done.2, f32[1,128]{1,0:T(1,128)S(1)} %bitcast.8, f32[1,64]{1,0:T(1,128)S(1)} %bitcast.9), custom_call_target="tpu_custom_call" | custom-call | flops 100663296 | bytes 1048576 | tf_op jit(solution)/shard_map/pallas_call | solution.py:234
  22.4 2.1 %collective-permute-done.refs_0_ = f32[4,64,128]{2,1,0:T(8,128)S(1)} collective-permute-done((f32[4,64,128]{2,1,0:T(8,128)S(1)}, f32[4,64,128]{2,1,0:T(8,128)S(1)}, u32[]{:S(2)}, u32[]{:S(2)}) %collective-permute-start) | collective-permute-done | bytes 131104 | tf_op jit(solution)/shard_map/ppermute | solution.py:230
  24.4 1.2 %shard_map.76 = f32[2,8,64,64]{3,2,1,0:T(8,128)} custom-call(f32[4,64,128]{2,1,0:T(8,128)S(1)} %collective-permute-done.refs_0_, f32[2,8,64,64]{3,2,1,0:T(8,128)S(1)} %get-tuple-element.7.refs_1_, f32[8,64,64]{2,1,0:T(8,128)S(1)} %get-tuple-element.8.refs_2_, bf16[2,384,512]{2,1,0:T(8,128)(2,1)S(1)} %copy-done), custom_call_target="tpu_custom_call" | custom-call | flops 25165824 | bytes 1048576 | tf_op jit(solution)/shard_map/pallas_call | solution.py:247
Async XLA Ops:
  0.0 20.6 %copy-start = (bf16[2,384,512]{2,1,0:T(8,128)(2,1)S(1)}, bf16[2,384,512]{2,1,0:T(8,128)(2,1)}, u32[]{:S(2)}) copy-start(bf16[2,384,512]{2,1,0:T(8,128)(2,1)} %constant.8.clone.w_ref.refs_3_) | copy-start | bytes 2359300
  1.5 17.3 %copy-start.1 = (bf16[2,64,256]{2,1,0:T(8,128)(2,1)S(1)}, bf16[2,64,256]{2,1,0:T(8,128)(2,1)}, u32[]{:S(2)}) copy-start(bf16[2,64,256]{2,1,0:T(8,128)(2,1)} %constant.7.clone.h_ref) | copy-start | bytes 196612
  19.0 5.4 %collective-permute-start = (f32[4,64,128]{2,1,0:T(8,128)S(1)}, f32[4,64,128]{2,1,0:T(8,128)S(1)}, u32[]{:S(2)}, u32[]{:S(2)}) collective-permute-start(f32[4,64,128]{2,1,0:T(8,128)S(1)} %shard_map.74), channel_id=1, source_target_pairs={{0,1},{1,0},{2,3},{3,2},{4,5},{5,4},{6,7},{7,6},{8,9},{9,8},{10,11... | collective-permute-start | bytes 393224 | tf_op jit(solution)/shard_map/ppermute | solution.py:230
  20.6 0.7 %copy-start.2 = (f32[128]{0:T(128)S(1)}, f32[128]{0:T(128)}, u32[]{:S(2)}) copy-start(f32[128]{0:T(128)} %sx_ref.1) | copy-start | bytes 1540
  20.6 0.7 %copy-start.3 = (f32[128]{0:T(128)S(1)}, f32[128]{0:T(128)}, u32[]{:S(2)}) copy-start(f32[128]{0:T(128)} %param.9) | copy-start | bytes 1540
  20.6 0.7 %copy-start.4 = (f32[64]{0:T(128)S(1)}, f32[64]{0:T(128)}, u32[]{:S(2)}) copy-start(f32[64]{0:T(128)} %param.10) | copy-start | bytes 772
